TPU v7x, 32 devices: a whole 2x2x4 slice. The times are simulated.
32 devices in a mesh: dp: 2 (over x), tp: 4 (over z), sp: 4 (over y, core).
Axes of the slice: x: 2, y: 2, z: 4, core: 2. Of those that a mesh axis runs over, the one named last changes fastest.
Arguments:
- hidden: bfloat16 [32768, 2048], P(('dp', 'sp')), parts along dimension 0
- w_query: bfloat16 [2048, 2048], P(None, 'tp')
- w_key: bfloat16 [2048, 2048], P(None, 'tp')
- w_value: bfloat16 [2048, 2048], P(None, 'tp')
- w_out: bfloat16 [2048, 2048], P('tp')
- branch_bias: float32 [4, 8], replicated
Outputs:
- output: bfloat16 [32768, 2048], P(('dp', 'sp'), 'tp'), parts along dimension 0
There are 2 independent parts. A program takes and returns all parts, laid end to end along the dimension named above; an argument that names none is the same for every part.
All inputs are finite; a program needn't handle non-finite values.
Results may differ from a plain program's by a relative error of at most 0.00343.
Values are sent between devices in bfloat16 or wider.
A program may use at most 1 GiB of HBM per device.

v0:
```python
import jax
import jax.numpy as jnp
from jax import lax
from jax.sharding import PartitionSpec as P

SEG_BASE = 2048


def attend(q_sel, k_sel, v_sel, logit_scale):
    logits = jnp.einsum('hasd,hatd->hast', q_sel, k_sel, preferred_element_type=jnp.float32) * logit_scale
    row_max = jnp.max(logits, axis=-1, keepdims=True)
    weights = jnp.exp(logits - row_max)
    row_sum = jnp.sum(weights, axis=-1, keepdims=True)
    numer_sum = jnp.einsum('hast,hatd->hasd', weights.astype(jnp.bfloat16), v_sel, preferred_element_type=jnp.float32)
    return numer_sum / row_sum, (row_max + jnp.log(row_sum))[..., 0]


def solution(mesh):
    seq_size = mesh.shape['sp']
    head_groups = mesh.shape['tp']

    def device_fn(hidden, w_query, w_key, w_value, w_out, branch_bias):
        tokens, model_width = hidden.shape
        num_branches, num_heads = branch_bias.shape
        head_dim = model_width // num_heads
        local_heads = num_heads // head_groups
        logit_scale = head_dim ** -0.5
        head_start = lax.axis_index('tp') * local_heads
        head_ids = head_start + jnp.arange(local_heads)
        bias_local = lax.dynamic_slice_in_dim(branch_bias, head_start, local_heads, axis=1)

        def project(weight):
            return jnp.dot(hidden, weight, preferred_element_type=jnp.float32).astype(jnp.bfloat16).reshape(tokens, local_heads, head_dim)

        q_loc = project(w_query)
        k_loc = project(w_key)
        v_loc = project(w_value)
        for branch in range(num_branches):
            value_a8 = 2 ** branch
            seg_len = SEG_BASE * value_a8
            kept_rows = tokens // value_a8
            phase_ok = head_ids[:, None] % value_a8 == jnp.arange(value_a8)[None, :]
            phase_bf = phase_ok.astype(jnp.bfloat16)
            phase_f = phase_ok.astype(jnp.float32)

            def pick_rows(source):
                split_rows = source.reshape(kept_rows, value_a8, local_heads, head_dim)
                return jnp.einsum('sihd,hi->hsd', split_rows, phase_bf, preferred_element_type=jnp.float32).astype(jnp.bfloat16)

            q_sel = pick_rows(q_loc)
            k_sel = pick_rows(k_loc)
            v_sel = pick_rows(v_loc)
            if seg_len <= tokens:
                seg_shape = (local_heads, tokens // seg_len, SEG_BASE, head_dim)
                attn_out, log_norm = attend(q_sel.reshape(seg_shape), k_sel.reshape(seg_shape), v_sel.reshape(seg_shape), logit_scale)
            else:
                group_len = seg_len // tokens
                k_parts = [k_sel]
                v_parts = [v_sel]
                for shift_by in range(1, group_len):
                    pairs_list = [(source_dev, (source_dev // group_len) * group_len + (source_dev + shift_by) % group_len) for source_dev in range(seq_size)]
                    k_parts.append(lax.ppermute(k_sel, 'sp', pairs_list))
                    v_parts.append(lax.ppermute(v_sel, 'sp', pairs_list))
                k_seg = jnp.concatenate(k_parts, axis=1)[:, None]
                v_seg = jnp.concatenate(v_parts, axis=1)[:, None]
                attn_out, log_norm = attend(q_sel[:, None], k_seg, v_seg, logit_scale)
            out_full = jnp.einsum('hsd,hi->sihd', attn_out.reshape(local_heads, kept_rows, head_dim), phase_f).reshape(tokens, local_heads, head_dim)
            lse_full = jnp.einsum('hs,hi->sih', log_norm.reshape(local_heads, kept_rows), phase_f).reshape(tokens, local_heads)
            mask_full = jnp.broadcast_to(phase_ok.T[None], (kept_rows, value_a8, local_heads)).reshape(tokens, local_heads)
            branch_score = jnp.where(mask_full, lse_full + bias_local[branch][None, :], -jnp.inf)
            if branch == 0:
                run_num = out_full
                run_max = branch_score
                run_den = jnp.ones_like(branch_score)
            else:
                new_max = jnp.maximum(run_max, branch_score)
                keep_old = jnp.exp(run_max - new_max)
                take_new = jnp.exp(branch_score - new_max)
                run_num = run_num * keep_old[..., None] + out_full * take_new[..., None]
                run_den = run_den * keep_old + take_new
                run_max = new_max
        combined = (run_num / run_den[..., None]).astype(jnp.bfloat16).reshape(tokens, local_heads * head_dim)
        part_out = jnp.dot(combined, w_out, preferred_element_type=jnp.float32)
        reduced = lax.psum_scatter(part_out, 'tp', scatter_dimension=1, tiled=True)
        return reduced.astype(jnp.bfloat16)

    return jax.shard_map(device_fn, mesh=mesh, in_specs=(P(('dp', 'sp'), None), P(None, 'tp'), P(None, 'tp'), P(None, 'tp'), P('tp', None), P(None, None)), out_specs=P(('dp', 'sp'), 'tp'), check_vma=False)
```

profile of v0, /device:TPU:0, one launch (start us, length us, event | category | flops | bytes accessed | tf_op | source)
XLA Modules:
  0.0 1055.1 jit_solution(18061375093241613068)
XLA Ops:
  7.3 14.5 %convolution_convert_fusion = bf16[4096,512]{0,1:T(8,128)(2,1)} fusion(bf16[4096,2048]{1,0:T(8,128)(2,1)} %param.6, bf16[2048,512]{1,0:T(8,128)(2,1)} %param.9), kind=kOutput, calls=%fused_computation.37 | convolution fusion | flops 8592031744 | bytes 23068672 | tf_op jit(solution)/shard_map/dot_general | solution.py:33
  28.2 7.0 reshape_reshape.38
  43.0 13.9 %convolution_convert_fusion.1 = bf16[4096,512]{0,1:T(8,128)(2,1)} fusion(bf16[4096,2048]{1,0:T(8,128)(2,1)} %param.6, bf16[2048,512]{1,0:T(8,128)(2,1)S(1)} %copy-done.12), kind=kOutput, calls=%fused_computation.38 | convolution fusion | flops 8592031744 | bytes 23068672 | tf_op jit(solution)/shard_map/dot_general | solution.py:33
  63.4 7.0 reshape_reshape.37
  77.0 7.0 reshape_reshape.34
  84.0 14.4 %convolution_convert_fusion.2 = bf16[4096,512]{0,1:T(8,128)(2,1)} fusion(bf16[4096,2048]{1,0:T(8,128)(2,1)} %param.6, bf16[2048,512]{1,0:T(8,128)(2,1)} %param.7), kind=kOutput, calls=%fused_computation.39 | convolution fusion | flops 8592031744 | bytes 23068672 | tf_op jit(solution)/shard_map/dot_general | solution.py:33
  104.9 6.9 reshape_reshape.36
  111.8 6.9 reshape_reshape.33
  118.7 7.0 reshape_reshape.35
  125.7 6.9 reshape_reshape.31
  132.6 6.9 reshape_reshape.30
  139.5 6.9 reshape_reshape.32
  163.1 11.8 %fusion.48 = bf16[2,1,2048,256]{3,1,2,0:T(2,128)(2,1)} fusion(pred[2,2,1,1]{1,2,3,0:T(4,128)(4,1)S(1)} %copy.68, bf16[2048,2,2,256]{3,2,1,0:T(2,128)(2,1)} %reshape_reshape.31), kind=kOutput, calls=%fused_computation.63 | convolution fusion | flops 4194304 | bytes 6291460 | tf_op jit(solution)/shard_map/sihd,hi->hsd/dot_general | solution.py:48
  174.9 8.8 fusion.50
  189.8 15.4 %multiply_reduce_fusion.1 = (f32[2,2048]{1,0:T(2,128)S(1)}, f32[2,2048,2048]{1,2,0:T(8,128)}) fusion(bf16[2,1,2048,256]{3,1,2,0:T(2,128)(2,1)} %fusion.48, bf16[2,1,2048,256]{3,1,2,0:T(2,128)(2,1)S(1)} %fusion.50), kind=kOutput, calls=%fused_computation.8 | convolution fusion | flops 4311740416 | bytes 37765120 | tf_op jit(solution)/shard_map/hasd,hatd->hast/dot_general | solution.py:10
  205.2 13.5 %fusion.7 = f32[2,2048]{1,0:T(2,128)S(1)} fusion(f32[2,2048,2048]{1,2,0:T(8,128)} %get-tuple-element.28, f32[2,2048]{1,0:T(2,128)S(1)} %get-tuple-element.27), kind=kLoop, calls=%fused_computation.10 | loop fusion | flops 25161728 | bytes 33587200 | tf_op jit(solution)/shard_map/reduce_sum | solution.py:13
  218.7 17.8 %fusion.52 = f32[2,2048,256]{2,1,0:T(8,128)} fusion(f32[2,2048,2048]{1,2,0:T(8,128)} %get-tuple-element.28, f32[2,2048]{1,0:T(2,128)S(1)} %get-tuple-element.27, bf16[2,1,2048,256]{3,1,2,0:T(2,128)(2,1)} %fusion.46, f32[2,2048]{1,0:T(2,128)S(1)} %fusion.7), kind=kOutput, calls=%fused_computation.67 | convolution fusion | flops 4321181696 | bytes 39878656 | tf_op jit(solution)/shard_map/hast,hatd->hasd/dot_general | solution.py:14
  236.6 8.8 copy.52
  254.6 8.9 copy.53
  282.6 26.4 %multiply_reduce_fusion = (f32[2,2,2048]{2,1,0:T(2,128)S(1)}, f32[2,2,2048,2048]{2,3,1,0:T(8,128)}) fusion(bf16[2,2,2048,256]{3,2,1,0:T(8,128)(2,1)} %bitcast.179, bf16[2,2,2048,256]{3,2,1,0:T(8,128)(2,1)} %bitcast.180), kind=kOutput, calls=%fused_computation.1 | convolution fusion | flops 8623480832 | bytes 75530240 | tf_op jit(solution)/shard_map/hasd,hatd->hast/dot_general | solution.py:10
  308.9 21.4 %fusion = f32[2,2,2048]{2,1,0:T(2,128)S(1)} fusion(f32[2,2,2048,2048]{2,3,1,0:T(8,128)} %get-tuple-element.30, f32[2,2,2048]{2,1,0:T(2,128)S(1)} %get-tuple-element.29), kind=kLoop, calls=%fused_computation.2 | loop fusion | flops 50323456 | bytes 67174400 | tf_op jit(solution)/shard_map/reduce_sum | solution.py:13
  330.3 28.6 %fusion.27 = f32[2,2,2048,256]{3,2,1,0:T(8,128)} fusion(bf16[2,2,2048,256]{3,2,1,0:T(8,128)(2,1)} %bitcast.187, f32[2,2,2048,2048]{2,3,1,0:T(8,128)} %get-tuple-element.30, f32[2,2,2048]{2,1,0:T(2,128)S(1)} %get-tuple-element.29, f32[2,2,2048]{2,1,0:T(2,128)S(1)} %fusion), kind=kOutput, calls=%fused_computation.40 | convolution fusion | flops 8642363392 | bytes 79757312 | tf_op jit(solution)/shard_map/hast,hatd->hasd/dot_general | solution.py:14
  358.9 8.9 copy.46
  395.3 9.3 multiply_bitcast_fusion
  404.6 7.6 copy.91
  412.2 8.9 copy.65
  438.5 7.8 broadcast_multiply_fusion
  446.3 7.6 copy.90
  453.8 8.9 copy.59
  464.0 12.8 %fusion.24 = bf16[4096,512]{0,1:T(8,128)(2,1)S(1)} fusion(f32[4096,512]{0,1:T(8,128)} %copy.65, f32[4096,512]{0,1:T(8,128)} %copy.59, f32[4096,512]{0,1:T(8,128)} %copy.53, f32[2,1,4096,256]{2,3,0,1:T(8,128)} %copy.46, f32[4096,2]{0,1:T(2,128)S(1)} %get-tuple-element.5, f32[4096,2]{0,1:T(2,128)S(1)} %get-tuple-element.11, ...), kind=kLoop, calls=%fused_computation.33 | loop fusion | flops 23068672 | bytes 37978112 | tf_op jit(solution)/shard_map/convert_element_type | solution.py:82
  476.9 15.6 %fusion.107 = f32[4096,2048]{1,0:T(8,128)} fusion(bf16[4096,512]{0,1:T(8,128)(2,1)S(1)} %fusion.24, bf16[512,2048]{1,0:T(8,128)(2,1)S(1)} %copy-done), kind=kOutput, calls=%fused_computation.154 | convolution fusion | flops 8589934592 | bytes 39845888 | tf_op jit(solution)/shard_map/dot_general | solution.py:83
  492.5 549.6 %reduce-scatter.2.cloned.1.call-done = f32[4096,512]{1,0:T(8,128)} async-done(((f32[4096,2048]{1,0:T(8,128)}), f32[4096,512]{1,0:T(8,128)}) %reduce-scatter.2.cloned.1.call-update) | async-done | bytes 8388624 | tf_op jit(solution)/shard_map/reduce_scatter | solution.py:84
  (109 shorter events, 137.5 us)
Async XLA Ops:
  6.5 470.3 %copy-start = (bf16[512,2048]{1,0:T(8,128)(2,1)S(1)}, bf16[512,2048]{1,0:T(8,128)(2,1)}, u32[]{:S(2)}) copy-start(bf16[512,2048]{1,0:T(8,128)(2,1)} %param.10) | copy-start | bytes 6291460
  6.5 1035.6 %reduce-scatter.2.cloned.1.call-start = ((), (), s32[]{:S(2)}) async-start(), calls=%async_computation.1 | async-start | bytes 41943040 | tf_op jit(solution)/shard_map/reduce_scatter | solution.py:84
  35.1 7.9 copy-start.12
  39.6 348.0 %collective-permute-start.7 = (bf16[2,512,256]{2,1,0:T(8,128)(2,1)}, bf16[2,512,256]{2,1,0:T(8,128)(2,1)}, u32[]{:S(2)}, u32[]{:S(2)}) collective-permute-start(bf16[2,512,256]{2,1,0:T(8,128)(2,1)} %bitcast.172), channel_id=1, source_target_pairs={{0,3},{1,0},{2,1},{3,2},{4,7},{5,4},{6,5},{7,6},{8,11},{9,8},{10,9... | collective-permute-start | bytes 1572872 | tf_op jit(solution)/shard_map/ppermute | solution.py:63
  42.4 345.3 %collective-permute-start.6 = (bf16[2,512,256]{2,1,0:T(8,128)(2,1)}, bf16[2,512,256]{2,1,0:T(8,128)(2,1)}, u32[]{:S(2)}, u32[]{:S(2)}) collective-permute-start(bf16[2,512,256]{2,1,0:T(8,128)(2,1)} %bitcast.172), channel_id=1, source_target_pairs={{0,2},{1,3},{2,0},{3,1},{4,6},{5,7},{6,4},{7,5},{8,10},{9,11},{10,... | collective-permute-start | bytes 1572872 | tf_op jit(solution)/shard_map/ppermute | solution.py:63
  74.7 307.3 %collective-permute-start.4 = (bf16[2,512,256]{2,1,0:T(8,128)(2,1)}, bf16[2,512,256]{2,1,0:T(8,128)(2,1)}, u32[]{:S(2)}, u32[]{:S(2)}) collective-permute-start(bf16[2,512,256]{2,1,0:T(8,128)(2,1)} %bitcast.173), channel_id=1, source_target_pairs={{0,3},{1,0},{2,1},{3,2},{4,7},{5,4},{6,5},{7,6},{8,11},{9,8},{10,9... | collective-permute-start | bytes 1572872 | tf_op jit(solution)/shard_map/ppermute | solution.py:62
  74.8 307.7 %collective-permute-start.3 = (bf16[2,512,256]{2,1,0:T(8,128)(2,1)}, bf16[2,512,256]{2,1,0:T(8,128)(2,1)}, u32[]{:S(2)}, u32[]{:S(2)}) collective-permute-start(bf16[2,512,256]{2,1,0:T(8,128)(2,1)} %bitcast.173), channel_id=1, source_target_pairs={{0,2},{1,3},{2,0},{3,1},{4,6},{5,7},{6,4},{7,5},{8,10},{9,11},{10,... | collective-permute-start | bytes 1572872 | tf_op jit(solution)/shard_map/ppermute | solution.py:62
  76.5 306.1 %collective-permute-start.2 = (bf16[2,512,256]{2,1,0:T(8,128)(2,1)}, bf16[2,512,256]{2,1,0:T(8,128)(2,1)}, u32[]{:S(2)}, u32[]{:S(2)}) collective-permute-start(bf16[2,512,256]{2,1,0:T(8,128)(2,1)} %bitcast.173), channel_id=1, source_target_pairs={{0,1},{1,2},{2,3},{3,0},{4,5},{5,6},{6,7},{7,4},{8,9},{9,10},{10,1... | collective-permute-start | bytes 1572872 | tf_op jit(solution)/shard_map/ppermute | solution.py:62
  152.8 5.8 copy-start.13
  152.8 5.8 copy-start.4
  163.1 11.8 %copy-start.2 = (bf16[2048,2,2,256]{3,2,1,0:T(2,128)(2,1)S(1)}, bf16[2048,2,2,256]{3,2,1,0:T(2,128)(2,1)}, u32[]{:S(2)}) copy-start(bf16[2048,2,2,256]{3,2,1,0:T(2,128)(2,1)} %reshape_reshape.30) | copy-start | bytes 12582916
  174.9 8.8 copy-start.3
  358.9 9.0 copy-start.8
  367.9 6.6 copy-start.9
  367.9 6.7 copy-start.11
  367.9 7.6 copy-start.7
  367.9 7.7 copy-start.10
  367.9 8.1 copy-start.6
  367.9 8.1 copy-start.14
  376.1 6.4 copy-start.1
  376.1 6.9 copy-start.5
  382.0 8.6 collective-permute-start.5
  382.4 41.0 %collective-permute-start = (bf16[2,1024,256]{2,1,0:T(8,128)(2,1)S(1)}, bf16[2,1024,256]{2,1,0:T(8,128)(2,1)}, u32[]{:S(2)}, u32[]{:S(2)}) collective-permute-start(bf16[2,1024,256]{2,1,0:T(8,128)(2,1)S(1)} %bitcast.185), channel_id=1, source_target_pairs={{0,1},{1,0},{2,3},{3,2},{4,5},{5,4},{6,7},{7,6},{8,9},{9,8},{10,11... | collective-permute-start | bytes 3145736 | tf_op jit(solution)/shard_map/ppermute | solution.py:62
  382.6 48.5 %collective-permute-start.1 = (bf16[2,1024,256]{2,1,0:T(8,128)(2,1)}, bf16[2,1024,256]{2,1,0:T(8,128)(2,1)}, u32[]{:S(2)}, u32[]{:S(2)}) collective-permute-start(bf16[2,1024,256]{2,1,0:T(8,128)(2,1)} %bitcast.170), channel_id=1, source_target_pairs={{0,1},{1,0},{2,3},{3,2},{4,5},{5,4},{6,7},{7,6},{8,9},{9,8},{10,11... | collective-permute-start | bytes 3145736 | tf_op jit(solution)/shard_map/ppermute | solution.py:63
Sparse Core Ops, SparseCore 0:
  492.6 549.4 reduce-scatter.1
where the time goes:
time: 1060 us
  waiting for transfers between devices  553 us (52%)
  matrix products  212 us (20%)
  local copies, waits for them, and re-layouts  182 us (17%)
  other arithmetic  87.2 us (8%)
  between operations  14 us (1%)
    reduce_scatter x1, waiting for transfers between devices, device_fn(): reduced = lax.psum_scatter(part_out, 'tp', scatter_dimension=1, tiled=True)  550 us
    another operation x9, local copies, waits for them, and re-layouts, pick_rows(): split_rows = source.reshape(kept_rows, value_a8, local_heads, head_dim)  62.4 us
    dot_general x4, matrix products, attend(): jnp.einsum('hast,hatd->hasd', weights.astype(jnp.bfloat16), v_sel, prefer...  53.7 us
    dot_general x9, matrix products, pick_rows(): jnp.einsum('sihd,hi->hsd', split_rows, phase_bf, preferred_element_type=j...  51.2 us
    dot_general x4, matrix products, attend(): jnp.einsum('hasd,hatd->hast', q_sel, k_sel, preferred_element_type=jnp.fl...  49.1 us
    dot_general x3, matrix products, project(): jnp.dot(hidden, weight, preferred_element_type=jnp.float32)  42.8 us
    reduce_sum x4, other arithmetic, attend(): row_sum = jnp.sum(weights, axis=-1, keepdims=True)  39.8 us
    reshape x3, local copies, waits for them, and re-layouts, device_fn(): jnp.einsum('hsd,hi->sihd', attn_out.reshape(local_heads, kept_rows, head_...  26.8 us
  transfers between devices with their start and end apart: 9, of which 2 were waited for; matrix products, arithmetic and copies ran while one was open for 36% of the time, Pallas kernels for 0%

commit v1 on v0

v1 whole, which is shorter than its diff:
```python
import functools
import math

import jax
import jax.numpy as jnp
from jax import lax
from jax.experimental import pallas as pl
from jax.experimental.pallas import tpu as pltpu
from jax.sharding import PartitionSpec as P

MESH = pl.DeviceIdType.MESH
BF = jnp.bfloat16
F32 = jnp.float32
D = 256
REL = (0, 4, 2, 6, 1, 5, 3, 7)
PAIR = (0, 2, 1, 3)
KAPPA = math.log2(math.e) / 16.0
VMEM = 66_000_000


def nn(a, b):
    return lax.dot_general(a, b, (((1,), (0,)), ((), ())), preferred_element_type=F32)


def nt(a, b):
    return lax.dot_general(a, b, (((1,), (1,)), ((), ())), preferred_element_type=F32)


def params(**kw):
    return pltpu.CompilerParams(vmem_limit_bytes=VMEM, **kw)


def phase_matrix(transposed):
    r = lax.broadcasted_iota(jnp.int32, (256, 256), 1 if transposed else 0)
    p = lax.broadcasted_iota(jnp.int32, (256, 256), 0 if transposed else 1)
    k = r // 32
    return (p == (r % 32) * 8 + k // 2 + 4 * (k % 2)).astype(F32).astype(BF)


def permute_kernel(x_ref, o_ref, pm_ref):
    @pl.when(pl.program_id(0) + pl.program_id(1) == 0)
    def _():
        pm_ref[...] = phase_matrix(False)

    o_ref[...] = nn(pm_ref[...], x_ref[...]).astype(BF).reshape(o_ref.shape)


def permute(x):
    n, d = x.shape
    return pl.pallas_call(
        permute_kernel,
        grid=(n // 2048, 8),
        in_specs=[pl.BlockSpec((256, d), lambda s, j: (s * 8 + j, 0))],
        out_specs=pl.BlockSpec((None, 8, 32, d), lambda s, j: (s, 0, j, 0)),
        out_shape=jax.ShapeDtypeStruct((n // 2048, 8, 256, d), BF),
        scratch_shapes=[pltpu.VMEM((256, 256), BF)],
        compiler_params=params(),
        cost_estimate=pl.CostEstimate(flops=2 * n * d * 256, bytes_accessed=4 * n * d, transcendentals=0),
        name='permute',
    )(x)


def unpermute_kernel(y_ref, o_ref, pm_ref):
    @pl.when(pl.program_id(0) + pl.program_id(1) == 0)
    def _():
        pm_ref[...] = phase_matrix(True)

    for j in range(y_ref.shape[1] // 32):
        y = y_ref[:, j * 32:(j + 1) * 32, :].reshape(256, y_ref.shape[2])
        o_ref[j * 256:(j + 1) * 256, :] = nn(pm_ref[...], y).astype(BF)


def unpermute(y):
    s, _, _, c = y.shape
    return pl.pallas_call(
        unpermute_kernel,
        grid=(s, 2),
        in_specs=[pl.BlockSpec((None, 8, 128, c), lambda s, j: (s, 0, j, 0))],
        out_specs=pl.BlockSpec((1024, c), lambda s, j: (s * 2 + j, 0)),
        out_shape=jax.ShapeDtypeStruct((s * 2048, c), BF),
        scratch_shapes=[pltpu.VMEM((256, 256), BF)],
        compiler_params=params(),
        name='unpermute',
    )(y)


def project_kernel(ids_ref, x_ref, wq_ref, wk_ref, wv_ref, q_ref, kv_ref, *k3_ref, pair0):
    hh = pl.program_id(0)
    pair = pl.program_id(2) + pair0
    rel = jnp.where(pair == 1, 2, jnp.where(pair == 2, 1, pair))
    swap = ((ids_ref[0] + hh + rel) & 7) >> 2
    x = x_ref[...].reshape(512, x_ref.shape[-1])
    q = nn(x, wq_ref[...]).astype(BF)
    k = nn(x, wk_ref[...]).astype(BF)
    v = nn(x, wv_ref[...])
    for j in range(2):
        rank = j ^ swap
        rows = slice(j * 256, (j + 1) * 256)
        vt = v[rows].T.astype(BF)
        q_ref[rank] = q[rows]
        kv_ref[rank, 0] = k[rows]
        kv_ref[rank, 1] = vt
        if k3_ref:
            @pl.when(rank == 0)
            def _(rows=rows, vt=vt):
                k3_ref[0][0] = k[rows]
                k3_ref[0][1] = vt


def project(ids, xp, wq, wk, wv, pair0, pairs, heads):
    segs, d = xp.shape[0], xp.shape[3]

    def x_map(h, s, p, ids):
        pair = p + pair0
        rel = jnp.where(pair == 1, 2, jnp.where(pair == 2, 1, pair))
        return (s, (ids[0] + h + rel) & 3, 0, 0)

    w_spec = pl.BlockSpec((d, D), lambda h, s, p, ids: (0, h))
    out_specs = [
        pl.BlockSpec((None, None, 2, 256, D), lambda h, s, p, ids: (h, s, p, 0, 0)),
        pl.BlockSpec((None, None, 2, 2, 256, D), lambda h, s, p, ids: (h, s, p, 0, 0, 0)),
    ]
    out_shape = [
        jax.ShapeDtypeStruct((heads, segs, 2 * pairs, 256, D), BF),
        jax.ShapeDtypeStruct((heads, segs, 2 * pairs, 2, 256, D), BF),
    ]
    if pair0 == 0:
        out_specs.append(pl.BlockSpec((None, None, 2, 256, D), lambda h, s, p, ids: (h, s, 0, 0, 0)))
        out_shape.append(jax.ShapeDtypeStruct((heads, segs, 2, 256, D), BF))
    rows = segs * pairs * 512
    return pl.pallas_call(
        functools.partial(project_kernel, pair0=pair0),
        grid_spec=pltpu.PrefetchScalarGridSpec(
            num_scalar_prefetch=1,
            grid=(heads, segs, pairs),
            in_specs=[pl.BlockSpec((None, 2, 256, d), x_map), w_spec, w_spec, w_spec],
            out_specs=out_specs,
        ),
        out_shape=out_shape,
        compiler_params=params(),
        cost_estimate=pl.CostEstimate(flops=heads * rows * d * D * 6, bytes_accessed=heads * rows * d * 2 + 6 * heads * d * D, transcendentals=0),
        name='project',
    )(ids, xp, wq, wk, wv)


def attend(kind, a, w, beta, hh, q, kv_s, kvp_s, kvr_s, s_scr, sr_scr):
    o = 1 - w

    def local(seg, r, n):
        return (lambda: kv_s[hh, seg, r:r + n, 0].reshape(n * 256, D), lambda: [kv_s[hh, seg, r + i, 1] for i in range(n)], n)

    def pair(seg, r):
        return (lambda: kvp_s[hh, seg, r, 0], lambda: [kvp_s[hh, seg, r, 1]], 1)

    def remote(i):
        return (lambda: kvr_s[hh, i:i + 2, 0].reshape(512, D), lambda: [kvr_s[hh, i, 1], kvr_s[hh, i + 1, 1]], 2)

    b0, b01, b1, b012, b12, b2, b0123, b123, b23, b3 = [beta(i) for i in range(10)]
    lane = lax.broadcasted_iota(jnp.int32, (1, 512), 1)

    def mix(x0, x1):
        return jnp.where(lane < 256, x0, x1)

    extra = []
    if kind == 2:
        parts = [(local(w, r, 2), None) for r in range(0, 8, 2)]
    elif kind == 1:
        parts = [(local(w, 0, 2), b01), (local(w, 2, 2), b01), (local(w, 4, 2), b0), (local(w, 6, 2), b0), (local(o, 0, 2), b1), (local(o, 2, 2), b1)]
    else:
        parts = [(local(w, 2, 2), b01), (local(w, 4, 2), b0), (local(w, 6, 2), b0), (local(o, 2, 2), b1),
                 (local(w, 0, 1), mix(b0123, b012)), (local(w, 1, 1), b012), (local(o, 0, 1), mix(b123, b12)), (local(o, 1, 1), b12)]
        for seg in range(2):
            parts += [(pair(seg, 0), mix(b23, b2)), (pair(seg, 1), b2)]
        extra = [(remote(0), b3), (remote(2), b3)]

    top = None
    off = 0
    for (k, _, n), b in parts:
        s = nt(k(), q)
        s_scr[off:off + n * 256, :] = s
        t = jnp.max(s, axis=0, keepdims=True) * KAPPA
        if b is not None:
            t = t + b
        top = t if top is None else jnp.maximum(top, t)
        off += n * 256
    if extra:
        topx = top[:, :256]
        off = 0
        for (k, _, n), b in extra:
            s = nt(k(), q[:256])
            sr_scr[off:off + n * 256, :] = s
            topx = jnp.maximum(topx, jnp.max(s, axis=0, keepdims=True) * KAPPA + b)
            off += n * 256
        top = jnp.concatenate([topx, top[:, 256:]], axis=1)

    acc = den = None
    off = 0
    for (_, v, n), b in parts:
        shift = top if b is None else top - b
        e = jnp.exp2(s_scr[off:off + n * 256, :] * KAPPA - shift)
        l = jnp.sum(e, axis=0, keepdims=True)
        vt = v()
        o_part = nn(vt[0] if n == 1 else jnp.concatenate(vt, axis=1), e.astype(BF))
        acc = o_part if acc is None else acc + o_part
        den = l if den is None else den + l
        off += n * 256
    if extra:
        accx, denx = None, den[:, :256]
        off = 0
        for (_, v, n), b in extra:
            e = jnp.exp2(sr_scr[off:off + n * 256, :] * KAPPA - (top[:, :256] - b))
            denx = denx + jnp.sum(e, axis=0, keepdims=True)
            o_part = nn(jnp.concatenate(v(), axis=1), e.astype(BF))
            accx = o_part if accx is None else accx + o_part
            off += n * 256
        acc = jnp.concatenate([acc[:, :256] + accx, acc[:, 256:]], axis=1)
        den = jnp.concatenate([denx, den[:, 256:]], axis=1)
    return acc / den


def mix_kernel(beta_ref, q0_ref, q1_ref, kv0_ref, kv1_ref, kvp_ref, kva_ref, kvb_ref, wown_ref, wlo_ref, whi_ref, out_ref,
               q_s, kv_s, kvp_s, kvr_s, wo_s, o_s, r_s, s_scr, sr_scr, in_sem, w_sem, o_send, r_sem, y_send, y_recv, *, axes, steps):
    t = pl.program_id(0)
    tp = lax.axis_index('tp')
    side = tp // 2
    inner = (tp == 1) | (tp == 2)
    idx = lax.axis_index('dp') * 4 + lax.axis_index('sp')
    a0 = 2 * tp
    n_attn = 16

    def loads():
        out = []
        for i, (src, dst) in enumerate(((q0_ref, lambda: q_s.at[:, :, pl.ds(0, 2)]), (q1_ref, lambda: q_s.at[:, :, pl.ds(2, 6)]),
                                        (kv0_ref, lambda: kv_s.at[:, :, pl.ds(0, 2)]), (kv1_ref, lambda: kv_s.at[:, :, pl.ds(2, 6)]),
                                        (kvp_ref, lambda: kvp_s), (kva_ref, lambda: kvr_s.at[:, pl.ds(0, 2)]), (kvb_ref, lambda: kvr_s.at[:, pl.ds(2, 2)]))):
            out.append(pltpu.make_async_copy(src, dst(), in_sem.at[i]))
        return out

    def w_loads():
        out = []
        for c in range(4):
            v = c ^ tp
            out.append(pltpu.make_async_copy(wown_ref.at[:, pl.ds(c * 512, 512)], wo_s.at[0, :, pl.ds(pl.multiple_of(v * 512, 512), 512)], w_sem.at[c]))
        for g, ref in ((0, wlo_ref), (1, whi_ref)):
            for j, m in enumerate((0, 4, 2, 6)):
                col = idx ^ (m + g)
                v = (col // 2) ^ tp
                dst = pl.multiple_of(v * 512 + (col & 1) * 256, 256)
                for b in range(3):
                    out.append(pltpu.make_async_copy(ref.at[j, b], wo_s.at[1 + b, :, pl.ds(dst, 256)], w_sem.at[4 + g * 12 + j * 3 + b]))
        return out

    def o_copy(c, seg, src_v, dst_tp):
        return pltpu.make_async_remote_copy(
            src_ref=o_s.at[seg, pl.ds(2 * c, 2)], dst_ref=r_s.at[src_v, pl.ds(2 * c, 2)],
            send_sem=o_send.at[seg, c], recv_sem=r_sem.at[src_v, c], device_id={'tp': dst_tp}, device_id_type=MESH)

    def y_src(k, v):
        return o_s.at[side, k] if v == 0 else r_s.at[v - 1, k]

    def y_copy(k, v, seg):
        return pltpu.make_async_remote_copy(
            src_ref=y_src(k, v), dst_ref=out_ref.at[seg, k], send_sem=y_send.at[k, v], recv_sem=y_recv.at[seg, k],
            device_id={'tp': tp ^ v}, device_id_type=MESH)

    def y_local(k):
        return pltpu.make_async_copy(y_src(k, 0), out_ref.at[side, k], y_send.at[k, 0])

    @pl.when(t == 0)
    def _():
        for c in loads():
            c.start()
        for c in w_loads():
            c.start()
        barrier = pltpu.get_barrier_semaphore()
        for v in (1, 2, 3):
            pl.semaphore_signal(barrier, inc=1, device_id={'tp': tp ^ v}, device_id_type=MESH)
        pl.semaphore_wait(barrier, 3)
        for c in loads():
            c.wait()

    p_steps = [i for i, s in enumerate(steps) if s == 'P']
    is_p = functools.reduce(jnp.logical_or, [t == i for i in p_steps])
    p_done = sum(jnp.where(t > i, 1, 0) for i in p_steps)
    u = t - p_done
    c = u // 4
    seg = jnp.where((u & 3) < 2, 1 - side, side)
    hh = u & 1
    a = a0 + hh
    rel = (c - a) & 3
    w = seg
    projector = 1 + seg

    def run(kind):
        rank_pair = {0: 0, 1: 1}.get(kind)
        if rank_pair is None:
            rank_pair = jnp.where(rel == 1, 2, 3)
        q = q_s[hh, w, pl.ds(2 * rank_pair, 2)].reshape(512, D)
        ot = attend(kind, a, w, lambda i: beta_ref[i, hh], hh, q, kv_s, kvp_s, kvr_s, s_scr, sr_scr)
        swap = ((a + rel) & 7) >> 2
        for j in range(2):
            o_s[w, 2 * c + (j ^ swap), :, pl.ds(pl.multiple_of(hh * D, D), D)] = ot[:, j * 256:(j + 1) * 256].T.astype(BF)

    @pl.when(jnp.logical_not(is_p))
    def _():
        pl.when(rel == 0)(lambda: run(0))
        pl.when(rel == 2)(lambda: run(1))
        pl.when((rel & 1) == 1)(lambda: run(2))

        @pl.when((hh == 1) & (tp != projector))
        def _():
            v = tp ^ projector
            o_copy(c, seg, v - 1, projector).start()

    @pl.when(t == p_steps[0])
    def _():
        for cp in w_loads():
            cp.wait()

    @pl.when(is_p & inner)
    def _():
        k = p_done
        cc = k // 2

        @pl.when(k % 2 == 0)
        def _():
            for v in (1, 2, 3):
                o_copy(cc, side, v - 1, tp).wait_recv()

        y = nn(o_s[side, k], wo_s[0])
        for v in (1, 2, 3):
            y = y + nn(r_s[v - 1, k], wo_s[v])
        y = y.astype(BF)
        o_s[side, k] = y[:, 0:512]
        for v in (1, 2, 3):
            r_s[v - 1, k] = y[:, v * 512:(v + 1) * 512]
        y_local(k).start()
        for v in (1, 2, 3):
            y_copy(k, v, side).start()

    @pl.when(t == len(steps) - 1)
    def _():
        for sg in range(2):
            @pl.when(tp != 1 + sg)
            def _():
                for cc in range(4):
                    o_copy(cc, sg, (tp ^ (1 + sg)) - 1, 1 + sg).wait_send()
                for k in range(8):
                    y_copy(k, 1, sg).wait_recv()

        @pl.when(inner)
        def _():
            for k in range(8):
                y_local(k).wait()
                for v in (1, 2, 3):
                    y_copy(k, v, side).wait_send()


STEPS = ('A',) * 12 + ('P', 'P') + ('A',) * 4 + ('P',) * 6


def mix_and_project(axes, beta, q0, q1, kv0, kv1, kvp, kva, kvb, w_out, wlo, whi):
    anyspec = pl.BlockSpec(memory_space=pl.ANY)
    return pl.pallas_call(
        functools.partial(mix_kernel, axes=axes, steps=STEPS),
        grid=(len(STEPS),),
        in_specs=[pl.BlockSpec(memory_space=pltpu.SMEM)] + [anyspec] * 10,
        out_specs=anyspec,
        out_shape=jax.ShapeDtypeStruct((2, 8, 256, 512), BF),
        scratch_shapes=[
            pltpu.VMEM((2, 2, 8, 256, D), BF),
            pltpu.VMEM((2, 2, 8, 2, 256, D), BF),
            pltpu.VMEM((2, 2, 2, 2, 256, D), BF),
            pltpu.VMEM((2, 4, 2, 256, D), BF),
            pltpu.VMEM((4, 512, 2048), BF),
            pltpu.VMEM((2, 8, 256, 512), BF),
            pltpu.VMEM((3, 8, 256, 512), BF),
            pltpu.VMEM((4096, 512), F32),
            pltpu.VMEM((1024, 256), F32),
            pltpu.SemaphoreType.DMA((7,)),
            pltpu.SemaphoreType.DMA((28,)),
            pltpu.SemaphoreType.DMA((2, 4)),
            pltpu.SemaphoreType.DMA((3, 4)),
            pltpu.SemaphoreType.DMA((8, 4)),
            pltpu.SemaphoreType.DMA((2, 8)),
        ],
        compiler_params=params(collective_id=0, has_side_effects=True),
        cost_estimate=pl.CostEstimate(flops=100_000_000_000, bytes_accessed=40_000_000, transcendentals=0),
        name='mix',
    )(beta, q0, q1, kv0, kv1, kvp, kva, kvb, w_out, wlo, whi)


def solution(mesh):
    axes = tuple(mesh.axis_names)
    sp_size = mesh.shape['sp']
    tp_size = mesh.shape['tp']
    dp_size = mesh.shape['dp']

    def xor_perm(x, axis, m, only=None):
        n = mesh.shape[axis]
        pairs = [(i, i ^ m) for i in range(n) if only is None or (i ^ m) in only]
        return lax.ppermute(x, axis, pairs)

    def plane_gather(x):
        x = x[None]
        x = jnp.concatenate([x, xor_perm(x, 'dp', 1) if dp_size > 1 else x])
        x = jnp.concatenate([x, xor_perm(x, 'sp', 2)])
        return x, xor_perm(x, 'sp', 1)

    def device_fn(hidden, w_query, w_key, w_value, w_out, branch_bias):
        tp = lax.axis_index('tp')
        idx = lax.axis_index('dp') * sp_size + lax.axis_index('sp')
        heads = branch_bias.shape[1] // tp_size

        w_sl = lax.dynamic_slice_in_dim(w_out, idx * 256, 256, axis=1)
        w_sl = jnp.stack([xor_perm(w_sl, 'tp', v, (1, 2)) for v in (1, 2, 3)])
        wlo, whi = plane_gather(w_sl)

        b = lax.dynamic_slice_in_dim(branch_bias, tp * heads, heads, axis=1)
        sets = ((0,), (0, 1), (1,), (0, 1, 2), (1, 2), (2,), (0, 1, 2, 3), (1, 2, 3), (2, 3), (3,))
        beta = []
        for st in sets:
            rows = b[jnp.array(st)]
            m = jnp.max(rows, axis=0)
            beta.append((m + jnp.log(jnp.sum(jnp.exp(rows - m), axis=0))) * math.log2(math.e))
        beta = jnp.stack(beta)

        ids = jnp.stack([2 * tp]).astype(jnp.int32)
        xp = permute(hidden)
        q0, kv0, kv3 = project(ids, xp, w_query, w_key, w_value, 0, 1, heads)
        kvp = xor_perm(kv0, 'sp', 1)
        kva = xor_perm(kv3, 'sp', 2)
        q1, kv1 = project(ids, xp, w_query, w_key, w_value, 1, 3, heads)
        kvb = xor_perm(kva, 'sp', 1)
        y = mix_and_project(axes, beta, q0, q1, kv0, kv1, kvp, kva, kvb, w_out, wlo, whi)
        return unpermute(y)

    return jax.shard_map(device_fn, mesh=mesh, in_specs=(P(('dp', 'sp'), None), P(None, 'tp'), P(None, 'tp'), P(None, 'tp'), P('tp', None), P(None, None)), out_specs=P(('dp', 'sp'), 'tp'), check_vma=False)
```

time: 1060 us -> 331 us (0.31)
  waiting for transfers between devices: 553 us -> 43.5 us
  Pallas kernels: 0 us -> 258 us
  matrix products: 212 us -> 0 us
  local copies, waits for them, and re-layouts: 182 us -> 5.65 us
  other arithmetic: 87.2 us -> 6.46 us
  between operations: 14 us -> 0.17 us
    reduce_scatter x1 -> x0, waiting for transfers between devices: 550 us -> none  [device_fn(): reduced = lax.psum_scatter(part_out, 'tp', scatter_dimension=1, tiled=True)]
    pallas_call x0 -> x5, Pallas kernels: none -> 258 us  [the longest x1 193 us: mix_and_project(): pl.pallas_call(functools.partial(mix_kernel, axes=axes, steps=STEPS), gri...]
    dot_general x21 -> x0, matrix products: 212 us -> none  [the longest x4 53.7 us: attend(): jnp.einsum('hast,hatd->hasd', weights.astype(jnp.bfloat16), v_sel, prefer...]
    another operation x12 -> x4, local copies, waits for them, and re-layouts: 62.7 us -> 1.22 us  [the longest x1 1.21 us: device_fn(): beta = jnp.stack(beta)]
    ppermute x8 -> x9, waiting for transfers between devices: 3.02 us -> 43.5 us  [xor_perm(): return lax.ppermute(x, axis, pairs)]
    reduce_sum x4 -> x6, other arithmetic: 39.8 us -> 0.14 us  [device_fn(): jnp.sum(jnp.exp(rows - m), axis=0)]
    convert_element_type x6 -> x0, local copies, waits for them, and re-layouts: 38.4 us -> none  [the longest x3 19.4 us: project(): jnp.dot(hidden, weight, preferred_element_type=jnp.float32)]
    reshape x9 -> x0, local copies, waits for them, and re-layouts: 34.3 us -> none  [the longest x3 26.8 us: device_fn(): jnp.einsum('hsd,hi->sihd', attn_out.reshape(local_heads, kept_rows, head_...]
  transfers between devices with their start and end apart: 9 -> 9, of which waited for: 2 -> 4; matrix products, arithmetic and copies ran while one was open for 36% -> 3% of each run, Pallas kernels for 0% -> 18%
where the time goes in v1:
time: 331 us; the launch traced here: 327 us
  Pallas kernels  258 us (78%)
  waiting for transfers between devices  43.5 us (13%)
  starting transfers between devices  13.4 us (4%)
  other arithmetic  6.46 us (2%)
  local copies, waits for them, and re-layouts  5.65 us (2%)
    pallas_call x1, Pallas kernels, mix_and_project(): pl.pallas_call(functools.partial(mix_kernel, axes=axes, steps=STEPS), gri...  193 us
    ppermute x9, waiting for transfers between devices, xor_perm(): return lax.ppermute(x, axis, pairs)  43.5 us
    pallas_call x2, Pallas kernels, project(): pl.pallas_call(functools.partial(project_kernel, pair0=pair0), grid_spec=...  39.2 us
    pallas_call x1, Pallas kernels, permute(): pl.pallas_call(permute_kernel, grid=(n // 2048, 8), in_specs=[pl.BlockSpe...  20.3 us
    ppermute x9, starting transfers between devices, xor_perm(): return lax.ppermute(x, axis, pairs)  13.4 us
  transfers between devices with their start and end apart: 9, of which 4 were waited for; matrix products, arithmetic and copies ran while one was open for 3% of the time, Pallas kernels for 18%

profile of v1, /device:TPU:0, one launch (start us, length us, event | category | flops | bytes accessed | tf_op | source)
XLA Modules:
  0.0 326.9 jit_solution(9683099279502736210)
XLA Ops:
  0.0 1.0 constant_dynamic-slice_fusion
  1.0 0.7 collective-permute-start.5
  1.7 7.7 %collective-permute-start.4 = (bf16[512,256]{1,0:T(8,128)(2,1)S(1)}, bf16[512,256]{1,0:T(8,128)(2,1)S(1)}, u32[]{:S(2)}, u32[]{:S(2)}) collective-permute-start(bf16[512,256]{1,0:T(8,128)(2,1)S(1)} %constant_dynamic-slice_fusion), channel_id=1, source_target_pairs={{0,8},{12,4},{1,9},{13,5},{2,10},{14,6},{3,11},{15,7},{16,24},{28,... | collective-permute-start | bytes 786440 | tf_op jit(solution)/shard_map/ppermute | solution.py:402
  9.4 1.4 collective-permute-start.3
  10.8 5.4 %collective-permute-done.4 = bf16[512,256]{1,0:T(8,128)(2,1)S(1)} collective-permute-done((bf16[512,256]{1,0:T(8,128)(2,1)S(1)}, bf16[512,256]{1,0:T(8,128)(2,1)S(1)}, u32[]{:S(2)}, u32[]{:S(2)}) %collective-permute-start.4) | collective-permute-done | bytes 262176 | tf_op jit(solution)/shard_map/ppermute | solution.py:402
  16.2 4.1 %collective-permute-done.3 = bf16[512,256]{1,0:T(8,128)(2,1)S(1)} collective-permute-done((bf16[512,256]{1,0:T(8,128)(2,1)S(1)}, bf16[512,256]{1,0:T(8,128)(2,1)S(1)}, u32[]{:S(2)}, u32[]{:S(2)}) %collective-permute-start.3) | collective-permute-done | bytes 262176 | tf_op jit(solution)/shard_map/ppermute | solution.py:402
  20.2 0.1 maximum_bitcast_fusion
  20.3 1.6 collective-permute-start.6
  21.9 20.3 %permute.1.x_ref = bf16[2,8,256,2048]{3,2,1,0:T(8,128)(2,1)} custom-call(bf16[4096,2048]{1,0:T(8,128)(2,1)} %x_ref.1), custom_call_target="tpu_custom_call" | custom-call | flops 4294967296 | bytes 33554432 | tf_op jit(solution)/shard_map/permute/pallas_call | solution.py:50
  42.2 0.0 collective-permute-done.6
  42.2 2.4 pad_maximum_fusion.1
  44.6 1.5 collective-permute-start.7
  46.1 12.2 %project.2 = (bf16[2,2,2,256,256]{4,3,2,1,0:T(8,128)(2,1)}, bf16[2,2,2,2,256,256]{5,4,3,2,1,0:T(8,128)(2,1)}, bf16[2,2,2,256,256]{4,3,2,1,0:T(8,128)(2,1)}) custom-call(s32[1]{0:T(128)} %bitcast.6.ids_ref, bf16[2,8,256,2048]{3,2,1,0:T(8,128)(2,1)} %permute.1.x_ref, bf16[2048,512]{1,0:T(8,128)(2,1)} %wq_ref.3, bf16[2048,512]{1,0:T(8,128)(2,1)} %wk_ref.3, ...), custom_call_target="tpu_custom_call" | custom-call | flops 6442450944 | bytes 14680064 | tf_op jit(solution)/shard_map/project/pallas_call | solution.py:131
  58.3 0.0 collective-permute-start
  58.4 0.6 collective-permute-start.1
  58.9 0.1 constant_dynamic-slice_fusion.1
  59.0 0.6 gather_fusion.1
  59.6 0.6 gather_fusion
  60.2 0.6 gather_fusion.3
  60.8 0.6 gather_fusion.2
  61.4 0.6 gather_fusion.5
  62.0 0.0 copy-start.2
  62.1 19.8 %collective-permute-done.7 = bf16[2,3,512,256]{3,2,1,0:T(8,128)(2,1)} collective-permute-done((bf16[2,3,512,256]{3,2,1,0:T(8,128)(2,1)}, bf16[2,3,512,256]{3,2,1,0:T(8,128)(2,1)}, u32[]{:S(2)}, u32[]{:S(2)}) %collective-permute-start.7) | collective-permute-done | bytes 1572896 | tf_op jit(solution)/shard_map/ppermute | solution.py:402
  81.9 3.6 %pad_maximum_fusion.wlo_ref = bf16[4,3,512,256]{3,2,1,0:T(8,128)(2,1)} fusion(bf16[2,3,512,256]{3,2,1,0:T(8,128)(2,1)} %collective-permute-done.7, bf16[1,3,512,256]{3,2,1,0:T(8,128)(2,1)} %collective-permute-done.6, bf16[1,3,512,256]{3,2,1,0:T(8,128)(2,1)S(1)} %maximum_bitcast_fusion), kind=kLoop, calls=%fused_computation.6 | loop fusion | flops 3145728 | bytes 6291456 | tf_op jit(solution)/shard_map/concatenate | solution.py:407
  85.5 0.0 collective-permute-start.8
  85.6 0.6 gather_fusion.4
  86.2 1.2 stack.12.beta_ref
  87.4 14.2 %collective-permute-done.1.kva_ref = bf16[2,2,2,256,256]{4,3,2,1,0:T(8,128)(2,1)} collective-permute-done((bf16[2,2,2,256,256]{4,3,2,1,0:T(8,128)(2,1)}, bf16[2,2,2,256,256]{4,3,2,1,0:T(8,128)(2,1)}, u32[]{:S(2)}, u32[]{:S(2)}) %collective-permute-start.1) | collective-permute-done | bytes 1048608 | tf_op jit(solution)/shard_map/ppermute | solution.py:402
  101.7 27.0 %project.3 = (bf16[2,2,6,256,256]{4,3,2,1,0:T(8,128)(2,1)}, bf16[2,2,6,2,256,256]{5,4,3,2,1,0:T(8,128)(2,1)}) custom-call(s32[1]{0:T(128)} %bitcast.6.ids_ref, bf16[2,8,256,2048]{3,2,1,0:T(8,128)(2,1)} %permute.1.x_ref, bf16[2048,512]{1,0:T(8,128)(2,1)} %wq_ref.3, bf16[2048,512]{1,0:T(8,128)(2,1)} %wk_ref.3, bf16[2048,512]{1,0:T(8,128)(2,1)} %wv_ref.3), custom_call_target="tpu_custom_call" | custom-call | flops 19327352832 | bytes 31457280 | tf_op jit(solution)/shard_map/project/pallas_call | solution.py:131
  128.7 0.0 copy-start.1
  128.7 192.6 %mix.1.y_ref = bf16[2,8,256,512]{3,2,1,0:T(8,128)(2,1)} custom-call(f32[10,2]{1,0:T(8,128)} %stack.12.beta_ref, bf16[2,2,2,256,256]{4,3,2,1,0:T(8,128)(2,1)} %get-tuple-element.10.q0_ref, bf16[2,2,6,256,256]{4,3,2,1,0:T(8,128)(2,1)} %get-tuple-element.11.q1_ref, bf16[2,2,2,2,256,256]{5,4,3,2,1,0:T(8,128)(2,1)} %get-tuple-element.12.kv0_ref, ...), custom_call_target="tpu_custom_call" | custom-call | flops 99999997952 | bytes 40000000 | tf_op jit(solution)/shard_map/mix/pallas_call | solution.py:364
  321.3 5.6 %unpermute.1 = bf16[4096,512]{1,0:T(8,128)(2,1)} custom-call(bf16[2,8,256,512]{3,2,1,0:T(8,128)(2,1)} %mix.1.y_ref), custom_call_target="tpu_custom_call" | custom-call | tf_op jit(solution)/shard_map/unpermute/pallas_call | solution.py:75
  (38 shorter events, 0.4 us)
Async XLA Ops:
  0.0 58.9 %copy-start = (f32[4,8]{1,0:T(4,128)S(1)}, f32[4,8]{1,0:T(4,128)}, u32[]{:S(2)}) copy-start(f32[4,8]{1,0:T(4,128)} %param.21) | copy-start | bytes 388
  1.0 9.8 %collective-permute-start.5 = (bf16[512,256]{1,0:T(8,128)(2,1)S(1)}, bf16[512,256]{1,0:T(8,128)(2,1)S(1)}, u32[]{:S(2)}, u32[]{:S(2)}) collective-permute-start(bf16[512,256]{1,0:T(8,128)(2,1)S(1)} %constant_dynamic-slice_fusion), channel_id=1, source_target_pairs={{4,8},{8,4},{5,9},{9,5},{6,10},{10,6},{7,11},{11,7},{20,24},{24,20... | collective-permute-start | bytes 786440 | tf_op jit(solution)/shard_map/ppermute | solution.py:402
  1.7 14.5 %collective-permute-start.4 = (bf16[512,256]{1,0:T(8,128)(2,1)S(1)}, bf16[512,256]{1,0:T(8,128)(2,1)S(1)}, u32[]{:S(2)}, u32[]{:S(2)}) collective-permute-start(bf16[512,256]{1,0:T(8,128)(2,1)S(1)} %constant_dynamic-slice_fusion), channel_id=1, source_target_pairs={{0,8},{12,4},{1,9},{13,5},{2,10},{14,6},{3,11},{15,7},{16,24},{28,... | collective-permute-start | bytes 786440 | tf_op jit(solution)/shard_map/ppermute | solution.py:402
  9.4 10.9 %collective-permute-start.3 = (bf16[512,256]{1,0:T(8,128)(2,1)S(1)}, bf16[512,256]{1,0:T(8,128)(2,1)S(1)}, u32[]{:S(2)}, u32[]{:S(2)}) collective-permute-start(bf16[512,256]{1,0:T(8,128)(2,1)S(1)} %constant_dynamic-slice_fusion), channel_id=1, source_target_pairs={{0,4},{12,8},{1,5},{13,9},{2,6},{14,10},{3,7},{15,11},{16,20},{28,... | collective-permute-start | bytes 786440 | tf_op jit(solution)/shard_map/ppermute | solution.py:402
  20.3 21.8 %collective-permute-start.6 = (bf16[1,3,512,256]{3,2,1,0:T(8,128)(2,1)S(1)}, bf16[1,3,512,256]{3,2,1,0:T(8,128)(2,1)}, u32[]{:S(2)}, u32[]{:S(2)}) collective-permute-start(bf16[1,3,512,256]{3,2,1,0:T(8,128)(2,1)S(1)} %maximum_bitcast_fusion), channel_id=1, source_target_pairs={{0,16},{16,0},{1,17},{17,1},{2,18},{18,2},{3,19},{19,3},{4,20},{20... | collective-permute-start | bytes 2359304 | tf_op jit(solution)/shard_map/ppermute | solution.py:402
  44.6 37.3 %collective-permute-start.7 = (bf16[2,3,512,256]{3,2,1,0:T(8,128)(2,1)}, bf16[2,3,512,256]{3,2,1,0:T(8,128)(2,1)}, u32[]{:S(2)}, u32[]{:S(2)}) collective-permute-start(bf16[2,3,512,256]{3,2,1,0:T(8,128)(2,1)} %pad_maximum_fusion.1), channel_id=1, source_target_pairs={{0,2},{1,3},{2,0},{3,1},{4,6},{5,7},{6,4},{7,5},{8,10},{9,11},{10,... | collective-permute-start | bytes 4718600 | tf_op jit(solution)/shard_map/ppermute | solution.py:402
  46.1 14.7 %copy-start.4 = (s32[2]{0:T(128)S(1)}, s32[2]{0:T(128)}, u32[]{:S(2)}) copy-start(s32[2]{0:T(128)} %constant.171) | copy-start | bytes 28
  46.1 15.2 %copy-start.3 = (s32[2]{0:T(128)S(1)}, s32[2]{0:T(128)}, u32[]{:S(2)}) copy-start(s32[2]{0:T(128)} %constant.173) | copy-start | bytes 28
  58.3 70.3 %collective-permute-start = (bf16[2,2,2,2,256,256]{5,4,3,2,1,0:T(8,128)(2,1)}, bf16[2,2,2,2,256,256]{5,4,3,2,1,0:T(8,128)(2,1)}, u32[]{:S(2)}, u32[]{:S(2)}) collective-permute-start(bf16[2,2,2,2,256,256]{5,4,3,2,1,0:T(8,128)(2,1)} %get-tuple-element.12.kv0_ref), channel_id=1, source_target_pairs={{0,1},{1,0},{2,3},{3,2},{4,5},{5,4},{6,7},{7,6},{8,9},{9,8},{10,11... | collective-permute-start | bytes 6291464 | tf_op jit(solution)/shard_map/ppermute | solution.py:402
  58.4 43.3 %collective-permute-start.1 = (bf16[2,2,2,256,256]{4,3,2,1,0:T(8,128)(2,1)}, bf16[2,2,2,256,256]{4,3,2,1,0:T(8,128)(2,1)}, u32[]{:S(2)}, u32[]{:S(2)}) collective-permute-start(bf16[2,2,2,256,256]{4,3,2,1,0:T(8,128)(2,1)} %get-tuple-element.14), channel_id=1, source_target_pairs={{0,2},{1,3},{2,0},{3,1},{4,6},{5,7},{6,4},{7,5},{8,10},{9,11},{10,... | collective-permute-start | bytes 3145736 | tf_op jit(solution)/shard_map/ppermute | solution.py:402
  62.0 23.5 %copy-start.2 = (s32[3]{0:T(128)S(1)}, s32[3]{0:T(128)}, u32[]{:S(2)}) copy-start(s32[3]{0:T(128)} %constant.172) | copy-start | bytes 40
  85.5 43.2 %collective-permute-start.8 = (bf16[4,3,512,256]{3,2,1,0:T(8,128)(2,1)}, bf16[4,3,512,256]{3,2,1,0:T(8,128)(2,1)}, u32[]{:S(2)}, u32[]{:S(2)}) collective-permute-start(bf16[4,3,512,256]{3,2,1,0:T(8,128)(2,1)} %pad_maximum_fusion.wlo_ref), channel_id=1, source_target_pairs={{0,1},{1,0},{2,3},{3,2},{4,5},{5,4},{6,7},{7,6},{8,9},{9,8},{10,11... | collective-permute-start | bytes 9437192 | tf_op jit(solution)/shard_map/ppermute | solution.py:402
  101.7 27.0 %collective-permute-start.2 = (bf16[2,2,2,256,256]{4,3,2,1,0:T(8,128)(2,1)}, bf16[2,2,2,256,256]{4,3,2,1,0:T(8,128)(2,1)}, u32[]{:S(2)}, u32[]{:S(2)}) collective-permute-start(bf16[2,2,2,256,256]{4,3,2,1,0:T(8,128)(2,1)} %collective-permute-done.1.kva_ref), channel_id=1, source_target_pairs={{0,1},{1,0},{2,3},{3,2},{4,5},{5,4},{6,7},{7,6},{8,9},{9,8},{10,11... | collective-permute-start | bytes 3145736 | tf_op jit(solution)/shard_map/ppermute | solution.py:402
  128.7 198.2 %copy-start.1 = (f32[4,8]{1,0:T(4,128)S(1)}, f32[4,8]{1,0:T(4,128)}, u32[]{:S(2)}) copy-start(f32[4,8]{1,0:T(4,128)} %param.21) | copy-start | bytes 388

commit v2 on v0

v2 whole, which is shorter than its diff:
```python
import functools
import math

import jax
import jax.numpy as jnp
from jax import lax
from jax.experimental import pallas as pl
from jax.experimental.pallas import tpu as pltpu
from jax.sharding import PartitionSpec as P

MESH = pl.DeviceIdType.MESH
BF = jnp.bfloat16
F32 = jnp.float32
D = 256
KAPPA = math.log2(math.e) / 16.0
VMEM = 66_900_000
SLOT = (0, 4, 2, 6, 1, 5, 3, 7)


def nn(a, b):
    return lax.dot_general(a, b, (((1,), (0,)), ((), ())), preferred_element_type=F32)


def nt(a, b):
    return lax.dot_general(a, b, (((1,), (1,)), ((), ())), preferred_element_type=F32)


def params(**kw):
    return pltpu.CompilerParams(vmem_limit_bytes=VMEM, **kw)


def aligned(x, m):
    return pl.multiple_of(x, m)


def phase_matrix(transposed):
    r = lax.broadcasted_iota(jnp.int32, (256, 256), 1 if transposed else 0)
    p = lax.broadcasted_iota(jnp.int32, (256, 256), 0 if transposed else 1)
    k = r // 32
    return (p == (r % 32) * 8 + k // 2 + 4 * (k % 2)).astype(F32).astype(BF)


def unpermute_kernel(y_ref, o_ref, pm_ref):
    @pl.when(pl.program_id(0) + pl.program_id(1) == 0)
    def _():
        pm_ref[...] = phase_matrix(True)

    for j in range(y_ref.shape[1] // 32):
        y = y_ref[:, j * 32:(j + 1) * 32, :].reshape(256, y_ref.shape[2])
        o_ref[j * 256:(j + 1) * 256, :] = nn(pm_ref[...], y).astype(BF)


def unpermute(y):
    s, _, _, c = y.shape
    return pl.pallas_call(
        unpermute_kernel,
        grid=(s, 2),
        in_specs=[pl.BlockSpec((None, 8, 128, c), lambda s, j: (s, 0, j, 0))],
        out_specs=pl.BlockSpec((1024, c), lambda s, j: (s * 2 + j, 0)),
        out_shape=jax.ShapeDtypeStruct((s * 2048, c), BF),
        scratch_shapes=[pltpu.VMEM((256, 256), BF)],
        compiler_params=params(),
        name='unpermute',
    )(y)


def softmax_mix(q, parts, s_at):
    top = None
    for i, (k, _, n, b) in enumerate(parts):
        s = nt(k(), q)
        s_at(i)[...] = s
        t = jnp.max(s, axis=0, keepdims=True) * KAPPA
        if b is not None:
            t = t + b
        top = t if top is None else jnp.maximum(top, t)
    acc = den = None
    for i, (_, v, n, b) in enumerate(parts):
        shift = top if b is None else top - b
        e = jnp.exp2(s_at(i)[...] * KAPPA - shift)
        l = jnp.sum(e, axis=0, keepdims=True)
        o = nn(v(), e.astype(BF))
        acc = o if acc is None else acc + o
        den = l if den is None else den + l
    return acc / den


def main_kernel(beta_ref, x_ref, wk_ref, wv_ref, wq_ref, wout_ref, out_ref, lq_ref, lo_ref,
                xb, pm, xp, ws, q_s, kv_s, kvp_s, kvr_s, s_scr,
                x_sem, w_sem, wo_sem, lq_send, lq_recv, lo_zsend, lo_zrecv, lo_send, lo_recv,
                kvp_send, kvp_recv, kvr_send, kvr_recv, kvf_send, kvf_recv, o_send, o_recv, y_send, y_recv, ready, *, steps):
    dp, tp, sp = lax.axis_index('dp'), lax.axis_index('tp'), lax.axis_index('sp')
    idx = dp * 4 + sp
    side = tp // 2
    inner = (tp == 1) | (tp == 2)
    outer = jnp.logical_not(inner)
    W = (wk_ref, wv_ref, wq_ref)
    peer_x, peer_y, peer_c = {'dp': dp ^ 1}, {'sp': sp ^ 2}, {'sp': sp ^ 1}

    def remote(src, dst, ss, rs, dev):
        return pltpu.make_async_remote_copy(src_ref=src, dst_ref=dst, send_sem=ss, recv_sem=rs, device_id=dev, device_id_type=MESH)

    def lq_copy(t, src, dst, dev):
        return remote(lq_ref.at[src, t], lq_ref.at[dst, t], lq_send.at[t, dst], lq_recv.at[t, dst], dev)

    def lq_z(t):
        return remote(W[t].at[pl.ds(aligned(idx * 256, 256), 256), :], lq_ref.at[0, t], lq_send.at[t, 0], lq_recv.at[t, 0], {'tp': tp ^ 2})

    def lo_copy(u, src, dst, dev):
        return remote(lo_ref.at[src, u], lo_ref.at[dst, u], lo_send.at[u, dst], lo_recv.at[u, dst], dev)

    def lo_z(u, dst):
        v = tp ^ dst
        b = jnp.where(v == 2, 0, jnp.where(v == 1, 1, 2))
        far = 1 - dst // 2 if u == 0 else dst // 2
        return remote(wout_ref.at[:, pl.ds(aligned(far * 1024 + idx * 128, 128), 128)], lo_ref.at[0, u, b], lo_zsend.at[dst - 1, u], lo_zrecv.at[u, b], {'tp': dst})

    def ev_z(copy, p, wait):
        wait()
        copy(p, 0, 2, peer_y).start()
        copy(p, 0, 1, peer_x).start()
        copy(p, 0, 4, peer_c).start()

    def ev_xy(copy, p):
        copy(p, 0, 2, peer_y).wait_recv()
        copy(p, 2, 3, peer_x).start()
        copy(p, 2, 6, peer_c).start()
        copy(p, 0, 1, peer_x).wait_recv()
        copy(p, 1, 5, peer_c).start()

    def ev_x2(copy, p):
        copy(p, 2, 3, peer_x).wait_recv()
        copy(p, 3, 7, peer_c).start()

    def ev_done(copy, p):
        for s in range(4):
            copy(p, s, 4 + s, peer_c).wait_recv()

    def sends_done(copy, p):
        for src, dst, dev in ((0, 2, peer_y), (0, 1, peer_x), (0, 4, peer_c), (2, 3, peer_x), (2, 6, peer_c), (1, 5, peer_c), (3, 7, peer_c)):
            copy(p, src, dst, dev).wait_send()

    def lo_wait_z(u):
        def wait():
            for b in range(3):
                remote(lo_ref.at[0, u, b], lo_ref.at[0, u, b], lo_zsend.at[0, u], lo_zrecv.at[u, b], {'tp': tp}).wait_recv()
        return wait

    def w_load(t):
        return [pltpu.make_async_copy(lq_ref.at[s, t], ws.at[t, pl.ds(aligned((idx ^ m) * 256, 256), 256), :], w_sem.at[t, s]) for s, m in enumerate(SLOT)]

    def own_load(t):
        return pltpu.make_async_copy(W[t], ws.at[t], w_sem.at[t, 0])

    def wo_pos(col):
        return ((col // 512) ^ tp ^ 2) * 512 + col % 512

    def wo_own():
        out = []
        for r in range(2):
            for c in range(4):
                out.append(pltpu.make_async_copy(wout_ref.at[pl.ds(r * 256, 256), pl.ds(c * 512, 512)],
                                                 xp.at[0, r, :, pl.ds(aligned((c ^ tp ^ 2) * 512, 512), 512)], wo_sem.at[2, r * 4 + c, 0, 0]))
        return out

    def wo_load(u):
        out = []
        base = 1024 * (1 - side) if u == 0 else 1024 * side
        for s, m in enumerate(SLOT):
            pos = aligned(wo_pos(base + (idx ^ m) * 128), 128)
            for b in range(3):
                for r in range(2):
                    out.append(pltpu.make_async_copy(lo_ref.at[s, u, b, pl.ds(r * 256, 256)], xp.at[0, 2 + 2 * b + r, :, pl.ds(pos, 128)], wo_sem.at[u, s, b, r]))
        return out

    def kvp_copy(h):
        return remote(kv_s.at[h, pl.ds(0, 4)], kvp_s.at[h], kvp_send.at[h], kvp_recv.at[h], peer_c)

    def kvr_copy(h, s):
        return remote(kv_s.at[h, 2 * s], kvr_s.at[h, s], kvr_send.at[h, s], kvr_recv.at[h, s], peer_y)

    def kvf_copy(h, s):
        return remote(kvr_s.at[h, s], kvr_s.at[h, 2 + s], kvf_send.at[h, s], kvf_recv.at[h, s], peer_c)

    def kv_forward(hs):
        for h in hs:
            for s in range(2):
                kvr_copy(h, s).wait_recv()
                kvf_copy(h, s).start()

    def order(k):
        return 2 * (k % 4) + ((k // 4) ^ side)

    def o_copy(k):
        return remote(xp.at[1, k, :, pl.ds(0, 1024)], xp.at[1, k, :, pl.ds(1024, 1024)], o_send.at[k], o_recv.at[k], {'tp': tp ^ 1})

    def y_src(k, v):
        if v == 0:
            return xp.at[1, k, :, pl.ds(0, 512)]
        return ws.at[{2: 0, 3: 1, 1: 2}[v], pl.ds(aligned(k * 256, 256), 256), :]

    def y_copy(k, v, seg):
        return remote(y_src(k, v), out_ref.at[seg, k], y_send.at[k, v], y_recv.at[seg, k], {'tp': tp ^ v})

    def y_local(k):
        return pltpu.make_async_copy(y_src(k, 0), out_ref.at[side, k], y_send.at[k, 0])

    def x_copy(j):
        return pltpu.make_async_copy(x_ref.at[pl.ds(aligned(j * 256, 256), 256), :], xb.at[lax.rem(j, 4)], x_sem.at[lax.rem(j, 4)])

    for j in range(4):
        x_copy(j).start()
    for t in range(3):
        own_load(t).start()
    barrier = pltpu.get_barrier_semaphore()
    peers = [{'tp': tp ^ 1}, {'tp': tp ^ 2}, {'tp': tp ^ 3}, peer_x, peer_y, peer_c]
    for dev in peers:
        pl.semaphore_signal(barrier, inc=1, device_id=dev, device_id_type=MESH)
    pl.semaphore_wait(barrier, len(peers))
    for t in range(3):
        lq_z(t).start()
    for u in range(2):
        for dst in (1, 2):
            pl.when(tp != dst)(lambda u=u, dst=dst: lo_z(u, dst).start())

    pm[...] = phase_matrix(False)

    def permute_body(j, _):
        x_copy(j).wait()
        y = nn(pm[...], xb[lax.rem(j, 4)]).astype(BF).reshape(8, 32, 2048)
        xp[j // 8, :, pl.ds(aligned(lax.rem(j, 8) * 32, 32), 32), :] = y
        pl.when(j < 12)(lambda: x_copy(j + 4).start())
        return None

    lax.fori_loop(0, 16, permute_body, None)

    def rows_of(a, g):
        sigma = jnp.where(g < 4, g & 1, 0)
        pair = jnp.where(g < 4, g // 2, g - 2)
        rel = jnp.where(pair == 1, 2, jnp.where(pair == 2, 1, pair))
        x = xp[side ^ sigma, pl.ds(2 * ((a + rel) & 3), 2)].reshape(512, 2048)
        return x, ((a + rel) & 7) >> 2, pair, sigma

    def wcols(t, hh):
        return ws[t, :, pl.ds(aligned(hh * 256, 256), 256)]

    def put_k(h, g, swap, k):
        k = k.astype(BF)
        for j in range(2):
            kv_s[h, 2 * g + (j ^ swap), 0] = k[j * 256:(j + 1) * 256]

    def put_v(h, g, swap, v):
        for j in range(2):
            kv_s[h, 2 * g + (j ^ swap), 1] = v[j * 256:(j + 1) * 256].T.astype(BF)

    def put_q(h, pair, swap, q):
        q = q.astype(BF)
        for j in range(2):
            q_s[h, 2 * pair + (j ^ swap)] = q[j * 256:(j + 1) * 256]

    for t in range(3):
        own_load(t).wait()

    def own_body(i, _):
        hh, g = i & 1, i // 2
        x, swap, pair, sigma = rows_of(2 * tp + hh, g)
        put_k(hh, g, swap, nn(x, wcols(0, hh)))
        put_v(hh, g, swap, nn(x, wcols(1, hh)))
        pl.when(sigma == 0)(lambda: put_q(hh, pair, swap, nn(x, wcols(2, hh))))

        @pl.when(i == 3)
        def _():
            for h in range(2):
                kvp_copy(h).start()
            ev_z(lq_copy, 0, lambda: lq_z(0).wait_recv())

        @pl.when(i == 6)
        def _():
            ev_xy(lq_copy, 0)

        @pl.when(i == 8)
        def _():
            ev_z(lq_copy, 1, lambda: lq_z(1).wait_recv())
            for s in range(2):
                kvr_copy(0, s).start()

        @pl.when(i == 10)
        def _():
            ev_x2(lq_copy, 0)
        return None

    lax.fori_loop(0, 12, own_body, None)
    ev_done(lq_copy, 0)
    for c in w_load(0):
        c.start()
    for c in w_load(0):
        c.wait()

    a_par = 2 * (tp ^ 2)

    def k_body(i, _):
        hh, g = i & 1, i // 2
        x, swap, pair, sigma = rows_of(a_par + hh, g)
        put_k(2 + hh, g, swap, nn(x, wcols(0, hh)))

        @pl.when(i == 1)
        def _():
            ev_xy(lq_copy, 1)

        @pl.when(i == 6)
        def _():
            ev_z(lq_copy, 2, lambda: lq_z(2).wait_recv())
            for s in range(2):
                kvr_copy(1, s).start()
        return None

    lax.fori_loop(0, 12, k_body, None)
    ev_x2(lq_copy, 1)
    ev_done(lq_copy, 1)
    for c in w_load(1):
        c.start()
    for c in w_load(1):
        c.wait()

    def v_body(i, _):
        hh, g = i & 1, i // 2
        x, swap, pair, sigma = rows_of(a_par + hh, g)
        put_v(2 + hh, g, swap, nn(x, wcols(1, hh)))

        @pl.when(i == 3)
        def _():
            for h in range(2, 4):
                kvp_copy(h).start()

        @pl.when(i == 6)
        def _():
            ev_xy(lq_copy, 2)

        @pl.when((i == 8) & inner)
        def _():
            ev_z(lo_copy, 0, lo_wait_z(0))
        return None

    lax.fori_loop(0, 12, v_body, None)
    for h in range(2, 4):
        for s in range(2):
            kvr_copy(h, s).start()
    ev_x2(lq_copy, 2)
    ev_done(lq_copy, 2)
    for c in w_load(2):
        c.start()
    for c in w_load(2):
        c.wait()

    def q_body(i, _):
        hh, pair = i & 1, i // 2
        g = jnp.where(pair == 3, 5, 2 * pair)
        x, swap, pair, sigma = rows_of(a_par + hh, g)
        put_q(2 + hh, pair, swap, nn(x, wcols(2, hh)))

        @pl.when((i == 3) & inner)
        def _():
            ev_xy(lo_copy, 0)
        return None

    lax.fori_loop(0, 8, q_body, None)

    pl.when(inner)(lambda: pl.semaphore_signal(ready, inc=1, device_id={'tp': tp ^ 1}, device_id_type=MESH))
    pl.when(outer)(lambda: pl.semaphore_wait(ready, 1))
    for c in wo_own():
        c.start()
    kv_forward((0, 1))
    for h in range(4):
        kvp_copy(h).wait_recv()
    for h in range(2):
        for s in range(2):
            kvf_copy(h, s).wait_recv()

    n_steps = len(steps)
    n_tiles = sum(s == 'A' for s in steps)

    def count_before(t, kind):
        return sum(jnp.where(t > i, 1, 0) for i, s in enumerate(steps) if s == kind)

    def is_kind(t, kind):
        return functools.reduce(jnp.logical_or, [t == i for i, s in enumerate(steps) if s == kind])

    def attn_tile(e):
        late = e >= 16
        h = jnp.where(late, e - 14, e & 3)
        a = (2 * jnp.where(h < 2, tp, tp ^ 2) + (h & 1))
        c = jnp.where(late, a & 3, e // 4)
        rel = (c - a) & 3
        b0, b01, b1, b012, b12, b2, b0123, b123, b23, b3 = [beta_ref[i, h] for i in range(10)]

        def loc(i, n, b):
            if n == 1:
                return (lambda: kv_s[h, i, 0], lambda: kv_s[h, i, 1], 256, b)
            return (lambda: kv_s[h, i:i + 2, 0].reshape(512, D), lambda: jnp.concatenate([kv_s[h, i, 1], kv_s[h, i + 1, 1]], axis=1), 512, b)

        def par(ref, i, n, b):
            if n == 1:
                return (lambda: ref[h, i, 0], lambda: ref[h, i, 1], 256, b)
            return (lambda: ref[h, i:i + 2, 0].reshape(512, D), lambda: jnp.concatenate([ref[h, i, 1], ref[h, i + 1, 1]], axis=1), 512, b)

        def wide(i):
            return s_scr.at[pl.ds(i * 512, 512), :]

        def narrow(parts):
            at = []
            off = 0
            for p in parts:
                lane, row = (0, off) if off < 3072 else (256, off - 3072)
                at.append((row, p[2], lane))
                off += p[2]
            return lambda i: s_scr.at[pl.ds(at[i][0], at[i][1]), pl.ds(at[i][2], 256)]

        def put(k, ot):
            xp[1, k, :, pl.ds(aligned(h * D, D), D)] = ot.T.astype(BF)

        def both(ot):
            swap = ((a + rel) & 7) >> 2
            for j in range(2):
                put(2 * c + (j ^ swap), ot[:, j * 256:(j + 1) * 256])

        @pl.when((rel & 1) == 1)
        def _():
            q = q_s[h, pl.ds(jnp.where(rel == 1, 4, 6), 2)].reshape(512, D)
            both(softmax_mix(q, [loc(i, 2, None) for i in (0, 4, 8, 10)], wide))

        @pl.when(rel == 2)
        def _():
            q = q_s[h, 2:4].reshape(512, D)
            both(softmax_mix(q, [loc(0, 2, b01), loc(4, 2, b01), loc(8, 2, b0), loc(10, 2, b0), loc(2, 2, b1), loc(6, 2, b1)], wide))

        @pl.when((rel == 0) & jnp.logical_not(late))
        def _():
            parts = [loc(0, 2, b012), loc(4, 2, b01), loc(8, 2, b0), loc(10, 2, b0), loc(2, 2, b12), loc(6, 2, b1), par(kvp_s, 0, 2, b2), par(kvp_s, 2, 2, b2)]
            put(2 * c + ((a >> 2) ^ 1), softmax_mix(q_s[h, 1], parts, narrow(parts)))

        @pl.when((rel == 0) & (late | (h < 2)))
        def _():
            parts = [loc(0, 1, b0123), loc(1, 1, b012), loc(4, 2, b01), loc(8, 2, b0), loc(10, 2, b0), loc(2, 1, b123), loc(3, 1, b12), loc(6, 2, b1),
                     par(kvp_s, 0, 1, b23), par(kvp_s, 1, 1, b2), par(kvp_s, 2, 1, b23), par(kvp_s, 3, 1, b2), par(kvr_s, 0, 2, b3), par(kvr_s, 2, 2, b3)]
            put(2 * c + (a >> 2), softmax_mix(q_s[h, 0], parts, narrow(parts)))

        @pl.when(outer)
        def _():
            for j in range(4):
                pl.when(e == 4 * j + 3)(lambda j=j: o_copy(order(j)).start())

            @pl.when(e == n_tiles - 1)
            def _():
                for j in range(4, 8):
                    o_copy(order(j)).start()

    def step_body(t, _):
        @pl.when(is_kind(t, 'A'))
        def _():
            attn_tile(count_before(t, 'A'))

        for i, s in enumerate(steps):
            if s == 'W0':
                @pl.when((t == i) & inner)
                def _():
                    ev_x2(lo_copy, 0)
                    ev_done(lo_copy, 0)
                    for c in wo_load(0):
                        c.start()
                    ev_z(lo_copy, 1, lo_wait_z(1))
                    for c in wo_load(0):
                        c.wait()
                @pl.when(t == i)
                def _():
                    for c in wo_own():
                        c.wait()
            elif s == 'W1':
                @pl.when((t == i) & inner)
                def _():
                    ev_xy(lo_copy, 1)
            elif s == 'W2':
                @pl.when((t == i) & inner)
                def _():
                    ev_x2(lo_copy, 1)
                    ev_done(lo_copy, 1)
                    for c in wo_load(1):
                        c.start()
                    for c in wo_load(1):
                        c.wait()
            elif s == 'F':
                pl.when(t == i)(lambda: kv_forward((2, 3)))
            elif s == 'G':
                @pl.when(t == i)
                def _():
                    for h in (2, 3):
                        for z in range(2):
                            kvf_copy(h, z).wait_recv()

        @pl.when(is_kind(t, 'R') & inner)
        def _():
            k = order(count_before(t, 'R'))
            o_copy(k).wait_recv()
            y = nn(xp[1, k], xp[0, :, :, 0:1024].reshape(2048, 1024)).astype(BF)
            for v in (2, 3):
                ws[v - 2, pl.ds(aligned(k * 256, 256), 256), :] = y[:, (v - 2) * 512:(v - 1) * 512]
                y_copy(k, v, side).start()

        @pl.when(is_kind(t, 'L') & inner)
        def _():
            k = order(count_before(t, 'L'))
            y = nn(xp[1, k], xp[0, :, :, 1024:2048].reshape(2048, 1024)).astype(BF)
            ws[2, pl.ds(aligned(k * 256, 256), 256), :] = y[:, 512:1024]
            y_copy(k, 1, side).start()
            xp[1, k, :, 0:512] = y[:, 0:512]
            y_local(k).start()
        return None

    lax.fori_loop(0, n_steps, step_body, None)

    for t in range(3):
        lq_z(t).wait_send()
        sends_done(lq_copy, t)
    for u in range(2):
        for dst in (1, 2):
            pl.when(tp != dst)(lambda u=u, dst=dst: lo_z(u, dst).wait_send())
        pl.when(inner)(lambda u=u: sends_done(lo_copy, u))
    for h in range(4):
        kvp_copy(h).wait_send()
        for s in range(2):
            kvr_copy(h, s).wait_send()
            kvf_copy(h, s).wait_send()

    @pl.when(outer)
    def _():
        for k in range(8):
            o_copy(k).wait_send()

    @pl.when(inner)
    def _():
        for k in range(8):
            for v in (1, 2, 3):
                y_copy(k, v, side).wait_send()
            y_local(k).wait()

    for seg in range(2):
        @pl.when(tp != 1 + seg)
        def _():
            for k in range(8):
                y_copy(k, 1, seg).wait_recv()


STEPS = ('A',) * 8 + ('W0', 'A', 'A', 'R', 'W1', 'A', 'A', 'A', 'A', 'R', 'F', 'A', 'A', 'W2', 'L', 'G', 'A', 'A', 'R', 'L', 'R', 'L', 'R', 'L', 'R', 'L', 'R', 'L', 'R', 'L', 'L')


def main(beta, x, wk, wv, wq, w_out):
    assert sum(s == 'A' for s in STEPS) == 18 and sum(s == 'R' for s in STEPS) == 8 and sum(s == 'L' for s in STEPS) == 8
    anyspec = pl.BlockSpec(memory_space=pl.ANY)
    dma = pltpu.SemaphoreType.DMA
    return pl.pallas_call(
        functools.partial(main_kernel, steps=STEPS),
        in_specs=[pl.BlockSpec(memory_space=pltpu.SMEM)] + [anyspec] * 5,
        out_specs=[anyspec] * 3,
        out_shape=[jax.ShapeDtypeStruct((2, 8, 256, 512), BF), jax.ShapeDtypeStruct((8, 3, 256, 512), BF), jax.ShapeDtypeStruct((8, 2, 3, 512, 128), BF)],
        scratch_shapes=[
            pltpu.VMEM((4, 256, 2048), BF),
            pltpu.VMEM((256, 256), BF),
            pltpu.VMEM((2, 8, 256, 2048), BF),
            pltpu.VMEM((3, 2048, 512), BF),
            pltpu.VMEM((4, 8, 256, D), BF),
            pltpu.VMEM((4, 12, 2, 256, D), BF),
            pltpu.VMEM((4, 4, 2, 256, D), BF),
            pltpu.VMEM((4, 4, 2, 256, D), BF),
            pltpu.VMEM((3072, 512), F32),
            dma((4,)), dma((3, 8)), dma((3, 8, 3, 2)), dma((3, 8)), dma((3, 8)), dma((2, 2)), dma((2, 3)), dma((2, 8)), dma((2, 8)),
            dma((4,)), dma((4,)), dma((4, 2)), dma((4, 2)), dma((4, 2)), dma((4, 2)), dma((8,)), dma((8,)), dma((8, 4)), dma((2, 8)),
            pltpu.SemaphoreType.REGULAR,
        ],
        compiler_params=params(collective_id=0, has_side_effects=True),
        cost_estimate=pl.CostEstimate(flops=100_000_000_000, bytes_accessed=40_000_000, transcendentals=0),
        name='main',
    )(beta, x, wk, wv, wq, w_out)[0]


def solution(mesh):
    tp_size = mesh.shape['tp']

    def device_fn(hidden, w_query, w_key, w_value, w_out, branch_bias):
        tp = lax.axis_index('tp')
        heads = branch_bias.shape[1] // tp_size
        b = jnp.concatenate([lax.dynamic_slice_in_dim(branch_bias, t * heads, heads, axis=1) for t in (tp, tp ^ 2)], axis=1)
        sets = ((0,), (0, 1), (1,), (0, 1, 2), (1, 2), (2,), (0, 1, 2, 3), (1, 2, 3), (2, 3), (3,))
        beta = []
        for st in sets:
            rows = [b[i:i + 1] for i in st]
            m = functools.reduce(jnp.maximum, rows)
            beta.append((m + jnp.log(sum(jnp.exp(r - m) for r in rows))) * math.log2(math.e))
        beta = jnp.concatenate(beta)
        return unpermute(main(beta, hidden, w_key, w_value, w_query, w_out))

    return jax.shard_map(device_fn, mesh=mesh, in_specs=(P(('dp', 'sp'), None), P(None, 'tp'), P(None, 'tp'), P(None, 'tp'), P('tp', None), P(None, None)), out_specs=P(('dp', 'sp'), 'tp'), check_vma=False)
```

time: 1060 us -> 234 us (0.22)
  waiting for transfers between devices: 553 us -> 0 us
  Pallas kernels: 0 us -> 232 us
  matrix products: 212 us -> 0 us
  local copies, waits for them, and re-layouts: 182 us -> 1.81 us
  other arithmetic: 87.2 us -> 0.21 us
  between operations: 14 us -> 0.02 us
    reduce_scatter x1 -> x0, waiting for transfers between devices: 550 us -> none  [device_fn(): reduced = lax.psum_scatter(part_out, 'tp', scatter_dimension=1, tiled=True)]
    pallas_call x0 -> x2, Pallas kernels: none -> 232 us  [the longest x1 226 us: main(): pl.pallas_call(functools.partial(main_kernel, steps=STEPS), in_specs=[pl....]
    dot_general x21 -> x0, matrix products: 212 us -> none  [the longest x4 53.7 us: attend(): jnp.einsum('hast,hatd->hasd', weights.astype(jnp.bfloat16), v_sel, prefer...]
    another operation x12 -> x0, local copies, waits for them, and re-layouts: 62.7 us -> none  [the longest x9 62.4 us: pick_rows(): split_rows = source.reshape(kept_rows, value_a8, local_heads, head_dim)]
    reduce_sum x4 -> x0, other arithmetic: 39.8 us -> none  [attend(): row_sum = jnp.sum(weights, axis=-1, keepdims=True)]
    convert_element_type x6 -> x0, local copies, waits for them, and re-layouts: 38.4 us -> none  [the longest x3 19.4 us: project(): jnp.dot(hidden, weight, preferred_element_type=jnp.float32)]
    reshape x9 -> x0, local copies, waits for them, and re-layouts: 34.3 us -> none  [the longest x3 26.8 us: device_fn(): jnp.einsum('hsd,hi->sihd', attn_out.reshape(local_heads, kept_rows, head_...]
    unnamed x33 -> x2, local copies, waits for them, and re-layouts: 19.4 us -> 0.18 us
  transfers between devices with their start and end apart: 9 -> 0, of which waited for: 2 -> 0; matrix products, arithmetic and copies ran while one was open for 36% -> 0% of each run, Pallas kernels for 0% -> 0%
where the time goes in v2:
time: 234 us
  Pallas kernels  232 us (99%)
    pallas_call x1, Pallas kernels, main(): pl.pallas_call(functools.partial(main_kernel, steps=STEPS), in_specs=[pl....  226 us
    pallas_call x1, Pallas kernels, unpermute(): pl.pallas_call(unpermute_kernel, grid=(s, 2), in_specs=[pl.BlockSpec((Non...  5.6 us

profile of v2, /device:TPU:0, one launch (start us, length us, event | category | flops | bytes accessed | tf_op | source)
XLA Modules:
  0.0 233.6 jit_solution(18180033747799458819)
XLA Ops:
  0.0 0.8 constant_dynamic-slice_fusion.1
  0.8 0.1 copy.10
  0.9 0.1 copy.11
  1.0 0.1 add_multiply_fusion.6
  1.1 0.1 add_multiply_fusion
  1.2 0.1 concatenate.7
  1.3 0.7 copy.9.beta_ref
  2.0 225.9 %main.1 = (bf16[2,8,256,512]{3,2,1,0:T(8,128)(2,1)}, bf16[8,3,256,512]{3,2,1,0:T(8,128)(2,1)}, bf16[8,2,3,512,128]{4,3,2,1,0:T(8,128)(2,1)}) custom-call(f32[10,4]{1,0:T(8,128)} %copy.9.beta_ref, bf16[4096,2048]{1,0:T(8,128)(2,1)} %x_ref.1, bf16[2048,512]{1,0:T(8,128)(2,1)} %wk_ref.1, bf16[2048,512]{1,0:T(8,128)(2,1)} %wv_ref.1, bf16[2048,512]{1,0:T(8,128)(2,1)} %wq_ref.1, ...), custom_call_target="tpu_custom_call" | custom-call | flops 99999997952 | bytes 40000000 | tf_op jit(solution)/shard_map/main/pallas_call | solution.py:558
  228.0 5.6 %unpermute.1 = bf16[4096,512]{1,0:T(8,128)(2,1)} custom-call(bf16[2,8,256,512]{3,2,1,0:T(8,128)(2,1)} %get-tuple-element.6.y_ref), custom_call_target="tpu_custom_call" | custom-call | tf_op jit(solution)/shard_map/unpermute/pallas_call | solution.py:55
  (1 shorter events, 0.0 us)
